TPU v7x, 32 devices: a whole 2x2x4 slice. The times are simulated.
32 devices in a mesh: ta: 8 (over y, x, core), ga: 4 (over z).
Axes of the slice: x: 2, y: 2, z: 4, core: 2. Of those that a mesh axis runs over, the one named last changes fastest.
Arguments:
- snapshots: bfloat16 [1024, 4, 16384], P('ta', 'ga'), may hold values from -12 to 12
- block_starts: int32 [7], replicated, may hold values from 0 to 768
- kept_freqs: int32 [32], replicated, may hold values from 0 to 128
Outputs:
- spectra: bfloat16 [4, 7, 2, 32, 16384], P('ga', None, None, None, 'ta')
- power_step: float32 [4, 7, 2, 32, 16384], P('ga', None, None, None, 'ta')
All inputs are finite; a program needn't handle non-finite values.
Results may differ from a plain program's by a relative error of at most 0.0047.
Values may be sent and summed in bfloat16 or wider, within the bound.
A program may use at most 192 MiB of HBM per device.

v0:
```python
import math

import jax
import jax.numpy as jnp
from jax import lax
from jax.sharding import PartitionSpec as P

NFFT = 256
NB = 7
NF = 32


def kernel_table(kept_freqs, sample_index):
    phase_index = kept_freqs[:, None] * sample_index[None, :] % NFFT
    angle_val = 2.0 * math.pi / NFFT * phase_index.astype(jnp.float32)
    window = 0.5 - 0.5 * jnp.cos(2.0 * math.pi / NFFT * sample_index.astype(jnp.float32))
    norm_scale = 2.0 / math.sqrt(NFFT)
    real_rows = window[None, :] * jnp.cos(angle_val) * norm_scale
    imag_rows = -window[None, :] * jnp.sin(angle_val) * norm_scale
    return jnp.concatenate([real_rows, imag_rows], axis=0)


def transform(series, kernel_rows, block_starts):
    blocks = []
    for block_index in range(NB):
        segment = lax.dynamic_slice_in_dim(series, block_starts[block_index], NFFT, 0)
        blocks.append(jnp.dot(kernel_rows, segment, preferred_element_type=jnp.float32))
    return jnp.stack(blocks).astype(jnp.bfloat16)


def gram_terms(spectra):
    values = spectra.reshape(NB, 2, NF, -1)
    real_part = values[:, 0]
    imag_part = values[:, 1]
    f32 = jnp.float32
    gram_re = jnp.einsum(
        "bfp,cfp->fbc", real_part, real_part, preferred_element_type=f32
    ) + jnp.einsum("bfp,cfp->fbc", imag_part, imag_part, preferred_element_type=f32)
    gram_im = jnp.einsum(
        "bfp,cfp->fbc", real_part, imag_part, preferred_element_type=f32
    ) - jnp.einsum("bfp,cfp->fbc", imag_part, real_part, preferred_element_type=f32)
    return (gram_re, gram_im)


def power_apply(spectra, gram_re, gram_im):
    values = spectra.astype(jnp.float32).reshape(NB, 2, NF, -1)
    real_part = values[:, 0]
    imag_part = values[:, 1]
    highest = lax.Precision.HIGHEST
    out_re = jnp.einsum("cfp,fcb->bfp", real_part, gram_re, precision=highest) - jnp.einsum(
        "cfp,fcb->bfp", imag_part, gram_im, precision=highest
    )
    out_im = jnp.einsum("cfp,fcb->bfp", real_part, gram_im, precision=highest) + jnp.einsum(
        "cfp,fcb->bfp", imag_part, gram_re, precision=highest
    )
    return jnp.stack([out_re, out_im], axis=1)


def shards(snapshots, block_starts, kept_freqs):
    ta_count = lax.axis_size("ta")
    ga_count = lax.axis_size("ga")
    local_times = snapshots.shape[0]
    own_pts = snapshots.shape[2] // ta_count
    kernel_rows = kernel_table(kept_freqs, jnp.arange(NFFT, dtype=jnp.int32)).astype(jnp.bfloat16)
    shaped = snapshots.reshape(local_times, ta_count, own_pts)
    arrived = lax.all_to_all(shaped, "ta", split_axis=1, concat_axis=0, tiled=True)
    spectra = transform(
        arrived.reshape(arrived.shape[0], arrived.shape[2]), kernel_rows, block_starts
    )
    late_sums = gram_terms(spectra)
    summed = lax.psum((late_sums[0], late_sums[1]), ("ta", "ga"))
    denominator = float(NB * own_pts * ta_count * ga_count)
    gram_re = summed[0] / denominator
    gram_im = summed[1] / denominator
    power = power_apply(spectra, gram_re, gram_im)
    return (spectra.reshape(1, NB, 2, NF, own_pts), power.reshape(1, NB, 2, NF, own_pts))


def solution(mesh):
    in_specs = (P("ta", "ga", None), P(), P())
    out_specs = (P("ga", None, None, None, "ta"), P("ga", None, None, None, "ta"))
    return jax.shard_map(shards, mesh=mesh, in_specs=in_specs, out_specs=out_specs, check_vma=False)
```

profile of v0, /device:TPU:0, one launch (start us, length us, event | category | flops | bytes accessed | tf_op | source)
XLA Modules:
  0.0 161.5 jit_solution(14835817679543147446)
XLA Ops:
  0.6 6.4 %copy.43 = bf16[128,1,16384]{0,2,1:T(8,128)(2,1)} copy(bf16[128,1,16384]{2,0,1:T(8,128)(2,1)} %param.3) | data formatting | bytes 8388608 | tf_op args[0]
  7.1 5.3 %all-to-all-start = ((bf16[128,8,2048]{0,2,1:T(8,128)(2,1)}), bf16[128,8,2048]{0,2,1:T(8,128)(2,1)}, u32[]{:S(2)}, u32[]{:S(2)}) async-start(bf16[128,8,2048]{0,2,1:T(8,128)(2,1)} %bitcast.61), calls=%async_computation | async-start | bytes 8388608 | tf_op jit(solution)/shard_map/all_to_all | solution.py:66
  26.4 35.2 %all-to-all-done = bf16[128,8,2048]{0,2,1:T(8,128)(2,1)} async-done(((bf16[128,8,2048]{0,2,1:T(8,128)(2,1)}), bf16[128,8,2048]{0,2,1:T(8,128)(2,1)}, u32[]{:S(2)}, u32[]{:S(2)}) %all-to-all-start) | async-done | bytes 4194336 | tf_op jit(solution)/shard_map/all_to_all | solution.py:66
  61.6 6.5 %copy.44 = bf16[8,128,1,2048]{3,1,0,2:T(8,128)(2,1)} copy(bf16[8,128,1,2048]{1,3,0,2:T(8,128)(2,1)} %bitcast.2) | data formatting | bytes 8388608 | tf_op jit(solution)/shard_map/all_to_all | solution.py:66
  68.1 1.8 %convolution_convert_fusion = bf16[64,2048]{1,0:T(8,128)(2,1)S(1)} fusion(bf16[1024,2048]{1,0:T(8,128)(2,1)} %bitcast.54, s32[]{:T(128)S(6)} %select_n.35, bf16[32,256]{1,0:T(8,128)(2,1)S(1)} %get-tuple-element.20, bf16[32,256]{1,0:T(8,128)(2,1)S(1)} %get-tuple-element.19), kind=kOutput, calls=%fused_computation.5 | convolution fusion | flops 67305472 | bytes 1343492 | tf_op jit(solution)/shard_map/dot_general | solution.py:27
  69.9 1.7 %convolution_convert_fusion.1 = bf16[64,2048]{1,0:T(8,128)(2,1)S(1)} fusion(bf16[1024,2048]{1,0:T(8,128)(2,1)} %bitcast.55, s32[]{:T(128)S(6)} %select_n.34, bf16[32,256]{1,0:T(8,128)(2,1)S(1)} %get-tuple-element.20, bf16[32,256]{1,0:T(8,128)(2,1)S(1)} %get-tuple-element.19), kind=kOutput, calls=%fused_computation.6 | convolution fusion | flops 67305472 | bytes 1343492 | tf_op jit(solution)/shard_map/dot_general | solution.py:27
  71.6 1.7 %convolution_convert_fusion.2 = bf16[64,2048]{1,0:T(8,128)(2,1)S(1)} fusion(bf16[1024,2048]{1,0:T(8,128)(2,1)} %bitcast.56, s32[]{:T(128)S(6)} %select_n.33, bf16[32,256]{1,0:T(8,128)(2,1)S(1)} %get-tuple-element.20, bf16[32,256]{1,0:T(8,128)(2,1)S(1)} %get-tuple-element.19), kind=kOutput, calls=%fused_computation.7 | convolution fusion | flops 67305472 | bytes 1343492 | tf_op jit(solution)/shard_map/dot_general | solution.py:27
  73.2 1.6 %convolution_convert_fusion.3 = bf16[64,2048]{1,0:T(8,128)(2,1)S(1)} fusion(bf16[1024,2048]{1,0:T(8,128)(2,1)} %bitcast.57, s32[]{:T(128)S(6)} %select_n.32, bf16[32,256]{1,0:T(8,128)(2,1)S(1)} %get-tuple-element.20, bf16[32,256]{1,0:T(8,128)(2,1)S(1)} %get-tuple-element.19), kind=kOutput, calls=%fused_computation.8 | convolution fusion | flops 67305472 | bytes 1343492 | tf_op jit(solution)/shard_map/dot_general | solution.py:27
  76.2 1.2 copy.46
  77.4 1.2 copy.45
  78.6 1.2 copy.47
  79.8 1.2 copy.48
  81.0 1.2 copy.49
  82.2 1.2 copy.50
  83.4 1.2 copy.51
  84.6 9.9 %stack.64 = bf16[7,2,32,2048]{3,0,2,1:T(8,128)(2,1)S(1)} concatenate(bf16[1,2,32,2048]{3,0,2,1:T(2,128)(2,1)} %copy.45, bf16[1,2,32,2048]{3,0,2,1:T(2,128)(2,1)} %copy.46, bf16[1,2,32,2048]{3,0,2,1:T(2,128)(2,1)} %copy.47, bf16[1,2,32,2048]{3,0,2,1:T(2,128)(2,1)} %copy.48, bf16[1,2,32,2048]{3,0,2,1:T(2,128)(2,1)} %copy.49, bf16[1,2,32,2048]{3,0,2,1:T(2,128)(2,1)} %copy.50, ...), dimensions={0} | concatenate | bytes 3670016 | tf_op jit(solution)/shard_map/stack | solution.py:28
  94.5 1.4 fusion.11
  96.0 1.4 fusion.10
  97.4 1.4 fusion.14
  99.5 1.6 %copy.55 = f32[32,7,7]{0,2,1:T(8,128)} copy(f32[32,7,7]{2,1,0:T(8,128)} %fusion.11) | data formatting | bytes 12544 | tf_op jit(solution)/shard_map/bfp,cfp->fbc/dot_general | solution.py:39
  101.2 1.6 %copy.56 = f32[32,7,7]{0,2,1:T(8,128)} copy(f32[32,7,7]{2,1,0:T(8,128)} %fusion.10) | data formatting | bytes 12544 | tf_op jit(solution)/shard_map/bfp,cfp->fbc/dot_general | solution.py:41
  102.8 1.6 %copy.53 = f32[32,7,7]{0,2,1:T(8,128)} copy(f32[32,7,7]{2,1,0:T(8,128)} %fusion.14) | data formatting | bytes 12544 | tf_op jit(solution)/shard_map/bfp,cfp->fbc/dot_general | solution.py:38
  106.7 41.2 %all-reduce = (f32[32,7,7]{0,2,1:T(8,128)S(1)}, f32[32,7,7]{0,2,1:T(8,128)S(1)}) all-reduce(f32[32,7,7]{0,2,1:T(8,128)S(1)} %sub.22, f32[32,7,7]{0,2,1:T(8,128)S(1)} %add.48), channel_id=1, replica_groups=mesh['ta'=8,'ga'=4] {'ta','ga'}, use_global_device_ids=true, to_apply=%region_1.2 | all-reduce | flops 3136 | bytes 25088 | tf_op jit(solution)/shard_map/psum | solution.py:71
  148.5 0.8 copy.54
  149.3 0.9 copy.57
  150.2 1.0 constant_dynamic-update-slice_fusion.6
  151.2 1.0 fusion.9
  152.2 1.0 fusion.12
  153.1 1.1 fusion
  154.3 1.1 fusion.1
  156.2 4.0 %copy.60 = f32[1,7,2,32,2048]{4,3,2,1,0:T(8,128)} copy(f32[1,7,2,32,2048]{4,1,3,2,0:T(8,128)S(1)} %maximum_bitcast_fusion) | data formatting | bytes 7340032
  160.3 1.2 copy-done.5
  (34 shorter events, 6.7 us)
Async XLA Ops:
  7.1 5.3 %copy-start.6 = (s32[7]{0:T(128)S(1)}, s32[7]{0:T(128)}, u32[]{:S(2)}) copy-start(s32[7]{0:T(128)} %param.4) | copy-start | bytes 88
  7.1 19.1 %copy-start.7 = (s32[32]{0:T(128)S(1)}, s32[32]{0:T(128)}, u32[]{:S(2)}) copy-start(s32[32]{0:T(128)} %param.5) | copy-start | bytes 388
  7.1 54.5 %all-to-all-start = ((bf16[128,8,2048]{0,2,1:T(8,128)(2,1)}), bf16[128,8,2048]{0,2,1:T(8,128)(2,1)}, u32[]{:S(2)}, u32[]{:S(2)}) async-start(bf16[128,8,2048]{0,2,1:T(8,128)(2,1)} %bitcast.61), calls=%async_computation | async-start | bytes 8388608 | tf_op jit(solution)/shard_map/all_to_all | solution.py:66
  68.1 6.8 %copy-start = (bf16[8,128,1,2048]{3,1,0,2:T(8,128)(2,1)S(1)}, bf16[8,128,1,2048]{3,1,0,2:T(8,128)(2,1)}, u32[]{:S(2)}) copy-start(bf16[8,128,1,2048]{3,1,0,2:T(8,128)(2,1)} %copy.44) | copy-start | bytes 12582916
  75.7 5.2 %copy-start.1 = (bf16[64,2048]{1,0:T(8,128)(2,1)}, bf16[64,2048]{1,0:T(8,128)(2,1)S(1)}, u32[]{:S(2)}) copy-start(bf16[64,2048]{1,0:T(8,128)(2,1)S(1)} %convolution_convert_fusion.5) | copy-start | bytes 786436
  76.2 7.2 %copy-start.3 = (bf16[64,2048]{1,0:T(8,128)(2,1)}, bf16[64,2048]{1,0:T(8,128)(2,1)S(1)}, u32[]{:S(2)}) copy-start(bf16[64,2048]{1,0:T(8,128)(2,1)S(1)} %convolution_convert_fusion.6) | copy-start | bytes 786436
  150.1 2.0 %copy-start.4 = (f32[32,7,7]{1,2,0:T(8,128)S(1)}, f32[32,7,7]{1,2,0:T(8,128)}, u32[]{:S(2)}) copy-start(f32[32,7,7]{1,2,0:T(8,128)} %copy.54) | copy-start | bytes 18820
  156.2 4.0 %copy-start.2 = (bf16[64,2048]{1,0:T(8,128)(2,1)S(1)}, bf16[64,2048]{1,0:T(8,128)(2,1)}, u32[]{:S(2)}) copy-start(bf16[64,2048]{1,0:T(8,128)(2,1)} %copy-done.1) | copy-start | bytes 786436
  160.3 1.2 copy-start.5
where the time goes:
time: 163 us; the launch traced here: 162 us
  local copies, waits for them, and re-layouts  45.6 us (28%)
  blocking collectives  41.2 us (25%)
  waiting for transfers between devices  35.2 us (22%)
  matrix products  17.2 us (11%)
  between operations  13.9 us (9%)
  starting transfers between devices  5.33 us (3%)
  other arithmetic  3.17 us (2%)
    psum x1, blocking collectives, shards(): summed = lax.psum((late_sums[0], late_sums[1]), ('ta', 'ga'))  41.2 us
    all_to_all x1, waiting for transfers between devices, shards(): lax.all_to_all(shaped, 'ta', split_axis=1, concat_axis=0, tiled=True)  35.2 us
    another operation x9, local copies, waits for them, and re-layouts, transform(): return jnp.stack(blocks).astype(jnp.bfloat16)  18.4 us
    unnamed x24, local copies, waits for them, and re-layouts  12.7 us
    dot_general x7, matrix products, transform(): jnp.dot(kernel_rows, segment, preferred_element_type=jnp.float32)  7.99 us
    all_to_all x1, local copies, waits for them, and re-layouts, shards(): lax.all_to_all(shaped, 'ta', split_axis=1, concat_axis=0, tiled=True)  6.54 us
    all_to_all x1, starting transfers between devices, shards(): lax.all_to_all(shaped, 'ta', split_axis=1, concat_axis=0, tiled=True)  5.33 us
  transfers between devices with their start and end apart: 1, of which 1 were waited for; matrix products, arithmetic and copies ran while one was open for 1% of the time, Pallas kernels for 0%

commit v1 on v0

v1 whole, which is shorter than its diff:
```python
import functools
import math

import jax
import jax.numpy as jnp
from jax import lax
from jax.experimental import pallas as pl
from jax.experimental.pallas import tpu as pltpu
from jax.sharding import PartitionSpec as P

NFFT = 256
MESH = pl.DeviceIdType.MESH
F32 = jnp.float32
BF16 = jnp.bfloat16


def kernel_table(kept_freqs, sample_index):
    phase_index = kept_freqs[:, None] * sample_index[None, :] % NFFT
    angle_val = 2.0 * math.pi / NFFT * phase_index.astype(F32)
    window = 0.5 - 0.5 * jnp.cos(2.0 * math.pi / NFFT * sample_index.astype(F32))
    norm_scale = 2.0 / math.sqrt(NFFT)
    real_rows = window[None, :] * jnp.cos(angle_val) * norm_scale
    imag_rows = -window[None, :] * jnp.sin(angle_val) * norm_scale
    return jnp.concatenate([real_rows, imag_rows], axis=0)


def round_up(value, step):
    return (value + step - 1) // step * step


def half_mask(nf, lanes):
    lane = lax.broadcasted_iota(jnp.int32, (8, lanes), 1)
    return lane % (2 * nf) < nf


def swap_halves(r, nf):
    lanes = r.shape[1]
    left = pltpu.roll(r, lanes - nf, 1)
    right = pltpu.roll(r, nf, 1)
    return jnp.where(half_mask(nf, lanes), left, right)


def diagonal(nf, lanes):
    row = lax.broadcasted_iota(jnp.int32, (nf, lanes), 0)
    lane = lax.broadcasted_iota(jnp.int32, (nf, lanes), 1)
    return lane % nf == row


def exchange_kernel(dims, x_ref, starts_ref, table_ref, spec_ref, cross_ref,
                    arrived, w_ref, spec, gram, rows_a, rows_b, slots_ta, slots_ga,
                    send_sem, recv_sem, own_sem, out_sem, sa_sem, ra_sem, sb_sem, rb_sem):
    n, nz, nb, nf, pts, chunks = dims
    me = lax.axis_index("ta")
    mz = lax.axis_index("ga")
    times = x_ref.shape[0]
    rows = nb * 2 * nf
    order = list(range(1, n))

    barrier = pltpu.get_barrier_semaphore()
    for o in order:
        pl.semaphore_signal(barrier, inc=1, device_id=(lax.rem(me + o, n), mz), device_id_type=MESH)
    for o in range(1, nz):
        pl.semaphore_signal(barrier, inc=1, device_id=(me, lax.rem(mz + o, nz)), device_id_type=MESH)
    pl.semaphore_wait(barrier, n - 1 + nz - 1)

    def piece(k, o):
        c0, cw = chunks[k]
        peer = lax.rem(me + o, n)
        src_col = pl.multiple_of(peer * pts + c0, 128)
        dst_row = pl.multiple_of(me * times, times)
        return pltpu.make_async_remote_copy(
            src_ref=x_ref.at[:, pl.ds(src_col, cw)],
            dst_ref=arrived.at[pl.ds(dst_row, times), pl.ds(c0, cw)],
            send_sem=send_sem.at[k, o],
            recv_sem=recv_sem.at[k, o],
            device_id=(peer, mz),
            device_id_type=MESH,
        )

    def own(k):
        c0, cw = chunks[k]
        src_col = pl.multiple_of(me * pts + c0, 128)
        dst_row = pl.multiple_of(me * times, times)
        return pltpu.make_async_copy(
            x_ref.at[:, pl.ds(src_col, cw)],
            arrived.at[pl.ds(dst_row, times), pl.ds(c0, cw)],
            own_sem.at[k],
        )

    for k in range(len(chunks)):
        for o in order:
            piece(k, o).start()
        own(k).start()

    total_times = n * times
    lag = (lax.broadcasted_iota(jnp.int32, (NFFT, total_times), 1)
           - lax.broadcasted_iota(jnp.int32, (NFFT, total_times), 0))

    def build(b, carry):
        shift = jnp.where(lag == starts_ref[b], 1.0, 0.0).astype(BF16)
        placed = jnp.dot(table_ref[...], shift, preferred_element_type=F32)
        w_ref[pl.ds(pl.multiple_of(b * 2 * nf, 2 * nf), 2 * nf), :] = placed.astype(BF16)
        return carry

    lax.fori_loop(0, nb, build, 0)
    gram[...] = jnp.zeros_like(gram)
    rows_a[...] = jnp.zeros_like(rows_a)
    rows_b[...] = jnp.zeros_like(rows_b)

    def out_copy(k):
        c0, cw = chunks[k]
        return pltpu.make_async_copy(
            spec.at[:, pl.ds(c0, cw)], spec_ref.at[:, pl.ds(c0, cw)], out_sem.at[k])

    for k, (c0, cw) in enumerate(chunks):
        own(k).wait()
        for o in order:
            piece(k, o).wait_recv()
        s = jnp.dot(w_ref[...], arrived[:, c0:c0 + cw], preferred_element_type=F32).astype(BF16)
        spec[:, c0:c0 + cw] = s
        out_copy(k).start()
        gram[:, :rows] += lax.dot_general(
            s, s, (((1,), (1,)), ((), ())), preferred_element_type=F32)

    lanes = gram.shape[1]
    keep = diagonal(nf, lanes)
    for b in range(nb):
        top = gram[2 * b * nf:(2 * b + 1) * nf, :]
        low = gram[(2 * b + 1) * nf:(2 * b + 2) * nf, :]
        rows_a[b:b + 1, :] = jnp.sum(jnp.where(keep, top, 0.0), axis=0, keepdims=True)
        rows_b[b:b + 1, :] = jnp.sum(jnp.where(keep, low, 0.0), axis=0, keepdims=True)
    swapped = swap_halves(rows_b[...], nf)
    local = rows_a[...] + jnp.where(half_mask(nf, lanes), swapped, -swapped)

    slots_ta[me] = local

    def stage_a(o):
        peer = lax.rem(me + o, n)
        return pltpu.make_async_remote_copy(
            src_ref=slots_ta.at[me], dst_ref=slots_ta.at[me],
            send_sem=sa_sem.at[o], recv_sem=ra_sem.at[o],
            device_id=(peer, mz), device_id_type=MESH)

    def stage_b(o):
        peer = lax.rem(mz + o, nz)
        return pltpu.make_async_remote_copy(
            src_ref=slots_ga.at[mz], dst_ref=slots_ga.at[mz],
            send_sem=sb_sem.at[o], recv_sem=rb_sem.at[o],
            device_id=(me, peer), device_id_type=MESH)

    for o in order:
        stage_a(o).start()
    for o in order:
        stage_a(o).wait_recv()
    plane = slots_ta[0]
    for i in range(1, n):
        plane = plane + slots_ta[i]
    slots_ga[mz] = plane
    for o in range(1, nz):
        stage_b(o).start()
    for o in range(1, nz):
        stage_b(o).wait_recv()
    whole = slots_ga[0]
    for i in range(1, nz):
        whole = whole + slots_ga[i]
    cross_ref[...] = whole

    for k in range(len(chunks)):
        out_copy(k).wait()
        for o in order:
            piece(k, o).wait_send()
    for o in order:
        stage_a(o).wait_send()
    for o in range(1, nz):
        stage_b(o).wait_send()


def power_kernel(dims, scale, cross_ref, spec_ref, spec_out, power_out, high, low):
    nb, nf = dims
    rows = nb * 2 * nf
    lanes = cross_ref.shape[1]

    @pl.when(pl.program_id(0) == 0)
    def _():
        cross = cross_ref[...] * scale
        swapped = swap_halves(cross, nf)
        turned = jnp.where(half_mask(nf, lanes), -swapped, swapped)
        keep = diagonal(nf, lanes)
        for b in range(nb):
            for c, source in enumerate((cross, turned)):
                m = jnp.where(keep, jnp.broadcast_to(source[b:b + 1, :], (nf, lanes)), 0.0)[:, :rows]
                hi = m.astype(BF16)
                r0 = (2 * b + c) * nf
                high[r0:r0 + nf, :] = hi
                low[r0:r0 + nf, :] = (m - hi.astype(F32)).astype(BF16)

    s = spec_ref[...]
    spec_out[...] = s
    power_out[...] = (jnp.dot(high[...], s, preferred_element_type=F32)
                      + jnp.dot(low[...], s, preferred_element_type=F32))


def shards(snapshots, block_starts, kept_freqs):
    n = lax.axis_size("ta")
    nz = lax.axis_size("ga")
    nb = block_starts.shape[0]
    nf = kept_freqs.shape[0]
    times = snapshots.shape[0]
    pts = snapshots.shape[2] // n
    rows = nb * 2 * nf
    lanes = round_up(rows, 128)
    assert nb <= 8
    width = pts // 4
    chunks = [(c0, width) for c0 in range(0, pts, width)]
    nk = len(chunks)
    table = kernel_table(kept_freqs, jnp.arange(NFFT, dtype=jnp.int32)).astype(BF16)
    x = snapshots.reshape(times, snapshots.shape[2])
    dma = pltpu.SemaphoreType.DMA
    spectra, cross = pl.pallas_call(
        functools.partial(exchange_kernel, (n, nz, nb, nf, pts, chunks)),
        out_shape=(jax.ShapeDtypeStruct((rows, pts), BF16),
                   jax.ShapeDtypeStruct((8, lanes), F32)),
        in_specs=[pl.BlockSpec(memory_space=pltpu.HBM),
                  pl.BlockSpec(memory_space=pltpu.SMEM),
                  pl.BlockSpec(memory_space=pltpu.VMEM)],
        out_specs=(pl.BlockSpec(memory_space=pl.ANY), pl.BlockSpec(memory_space=pltpu.VMEM)),
        scratch_shapes=[
            pltpu.VMEM((n * times, pts), BF16),
            pltpu.VMEM((rows, n * times), BF16),
            pltpu.VMEM((rows, pts), BF16),
            pltpu.VMEM((rows, lanes), F32),
            pltpu.VMEM((8, lanes), F32),
            pltpu.VMEM((8, lanes), F32),
            pltpu.VMEM((n, 8, lanes), F32),
            pltpu.VMEM((nz, 8, lanes), F32),
            dma((nk, n)), dma((nk, n)), dma((nk,)), dma((nk,)),
            dma((n,)), dma((n,)), dma((nz,)), dma((nz,)),
        ],
        compiler_params=pltpu.CompilerParams(
            collective_id=0, has_side_effects=True, vmem_limit_bytes=40 * 1024 * 1024),
        name="exchange",
    )(x, block_starts, table)

    tile = pts // 4
    spectra, power = pl.pallas_call(
        functools.partial(power_kernel, (nb, nf), 1.0 / float(nb * pts * n * nz)),
        grid=(pts // tile,),
        out_shape=(jax.ShapeDtypeStruct((rows, pts), BF16),
                   jax.ShapeDtypeStruct((rows, pts), F32)),
        in_specs=[pl.BlockSpec((8, lanes), lambda i: (0, 0)),
                  pl.BlockSpec((rows, tile), lambda i: (0, i))],
        out_specs=(pl.BlockSpec((rows, tile), lambda i: (0, i)),
                   pl.BlockSpec((rows, tile), lambda i: (0, i))),
        scratch_shapes=[pltpu.VMEM((rows, rows), BF16), pltpu.VMEM((rows, rows), BF16)],
        compiler_params=pltpu.CompilerParams(vmem_limit_bytes=32 * 1024 * 1024),
        name="power",
    )(cross, spectra)
    return (spectra.reshape(1, nb, 2, nf, pts), power.reshape(1, nb, 2, nf, pts))


def solution(mesh):
    in_specs = (P("ta", "ga", None), P(), P())
    out_specs = (P("ga", None, None, None, "ta"), P("ga", None, None, None, "ta"))
    return jax.shard_map(shards, mesh=mesh, in_specs=in_specs, out_specs=out_specs, check_vma=False)
```

time: 163 us -> 70.5 us (0.43)
  Pallas kernels: 0 us -> 65.9 us
  local copies, waits for them, and re-layouts: 45.6 us -> 2.84 us
  blocking collectives: 41.2 us -> 0 us
  waiting for transfers between devices: 35.2 us -> 0 us
  matrix products: 17.2 us -> 0 us
  between operations: 13.9 us -> 0.66 us
  starting transfers between devices: 5.33 us -> 0 us
  other arithmetic: 3.17 us -> 0.93 us
    pallas_call x0 -> x2, Pallas kernels: none -> 65.9 us  [the longest x1 61.8 us: shards(): pl.pallas_call(functools.partial(exchange_kernel, (n, nz, nb, nf, pts, ch...]
    psum x1 -> x0, blocking collectives: 41.2 us -> none  [shards(): summed = lax.psum((late_sums[0], late_sums[1]), ('ta', 'ga'))]
    all_to_all x1 -> x0, waiting for transfers between devices: 35.2 us -> none  [shards(): lax.all_to_all(shaped, 'ta', split_axis=1, concat_axis=0, tiled=True)]
    another operation x9 -> x0, local copies, waits for them, and re-layouts: 18.4 us -> none  [transform(): return jnp.stack(blocks).astype(jnp.bfloat16)]
    dot_general x15 -> x0, matrix products: 17.2 us -> none  [the longest x7 7.99 us: transform(): jnp.dot(kernel_rows, segment, preferred_element_type=jnp.float32)]
    unnamed x24 -> x4, local copies, waits for them, and re-layouts: 12.7 us -> 2.84 us
    all_to_all x1 -> x0, local copies, waits for them, and re-layouts: 6.54 us -> none  [shards(): lax.all_to_all(shaped, 'ta', split_axis=1, concat_axis=0, tiled=True)]
    dot_general x4 -> x0, local copies, waits for them, and re-layouts: 5.61 us -> none  [the longest x1 1.64 us: gram_terms(): jnp.einsum('bfp,cfp->fbc', real_part, imag_part, preferred_element_type=f32)]
  transfers between devices with their start and end apart: 1 -> 0, of which waited for: 1 -> 0; matrix products, arithmetic and copies ran while one was open for 1% -> 0% of each run, Pallas kernels for 0% -> 0%
where the time goes in v1:
time: 70.5 us; the launch traced here: 70.4 us
  Pallas kernels  65.9 us (93%)
  local copies, waits for them, and re-layouts  2.84 us (4%)
  other arithmetic  0.93 us (1%)
    pallas_call x1, Pallas kernels, shards(): pl.pallas_call(functools.partial(exchange_kernel, (n, nz, nb, nf, pts, ch...  61.8 us
    pallas_call x1, Pallas kernels, shards(): pl.pallas_call(functools.partial(power_kernel, (nb, nf), 1.0 / float(nb *...  4.1 us
    unnamed x4, local copies, waits for them, and re-layouts  2.84 us

profile of v1, /device:TPU:0, one launch (start us, length us, event | category | flops | bytes accessed | tf_op | source)
XLA Modules:
  0.0 70.4 jit_solution(867659571658594333)
XLA Ops:
  0.7 0.9 %multiply_convert_fusion.1 = (bf16[32,256]{1,0:T(8,128)(2,1)S(1)}, bf16[32,256]{1,0:T(8,128)(2,1)S(1)}) fusion(s32[32]{0:T(128)} %param.5, f32[256]{0:T(256)S(1)} %get-tuple-element.12, f32[256]{0:T(256)S(1)} %get-tuple-element.13), kind=kLoop, calls=%fused_computation.8 | loop fusion | flops 163840 | bytes 34944 | tf_op jit(solution)/shard_map/convert
  1.6 0.0 copy-start
  1.6 2.2 %copy-done = bf16[128,1,16384]{2,0,1:T(8,128)(2,1)S(1)} copy-done((bf16[128,1,16384]{2,0,1:T(8,128)(2,1)S(1)}, bf16[128,1,16384]{2,0,1:T(8,128)(2,1)}, u32[]{:S(2)}) %copy-start) | copy-done | bytes 4194328
  3.8 0.0 copy-start.1
  3.8 0.7 copy-done.1
  4.4 61.8 %exchange.1 = (bf16[448,2048]{1,0:T(8,128)(2,1)S(1)}, f32[8,512]{1,0:T(8,128)S(1)}) custom-call(bf16[128,16384]{1,0:T(8,128)(2,1)S(1)} %bitcast.3, s32[7]{0:T(128)S(1)} %copy-done.1, bf16[64,256]{1,0:T(8,128)(2,1)S(1)} %pad_maximum_fusion.table_ref), custom_call_target="tpu_custom_call" | custom-call | tf_op jit(solution)/shard_map/exchange/pallas_call | solution.py:219
  66.3 4.1 %power.1 = (bf16[448,2048]{1,0:T(8,128)(2,1)}, f32[448,2048]{1,0:T(8,128)}) custom-call(f32[8,512]{1,0:T(8,128)S(1)} %get-tuple-element.6.cross_ref, bf16[448,2048]{1,0:T(8,128)(2,1)S(1)} %get-tuple-element.7.spec_ref), custom_call_target="tpu_custom_call" | custom-call | tf_op jit(solution)/shard_map/power/pallas_call | solution.py:245
  (2 shorter events, 0.1 us)
Async XLA Ops:
  1.6 2.2 %copy-start = (bf16[128,1,16384]{2,0,1:T(8,128)(2,1)S(1)}, bf16[128,1,16384]{2,0,1:T(8,128)(2,1)}, u32[]{:S(2)}) copy-start(bf16[128,1,16384]{2,0,1:T(8,128)(2,1)} %param.3) | copy-start | bytes 12582916
  3.8 0.7 copy-start.1

commit v2 on v1

--- a/solution.py
+++ b/solution.py
@@ -14,14 +14,20 @@
 BF16 = jnp.bfloat16
 
 
-def kernel_table(kept_freqs, sample_index):
-    phase_index = kept_freqs[:, None] * sample_index[None, :] % NFFT
-    angle_val = 2.0 * math.pi / NFFT * phase_index.astype(F32)
-    window = 0.5 - 0.5 * jnp.cos(2.0 * math.pi / NFFT * sample_index.astype(F32))
-    norm_scale = 2.0 / math.sqrt(NFFT)
-    real_rows = window[None, :] * jnp.cos(angle_val) * norm_scale
-    imag_rows = -window[None, :] * jnp.sin(angle_val) * norm_scale
-    return jnp.concatenate([real_rows, imag_rows], axis=0)
+def build_table(phase, freqs, table):
+    nf, nfft = phase.shape
+    sample = lax.broadcasted_iota(jnp.int32, (1, nfft), 1)
+
+    def phase_row(j, carry):
+        phase[pl.ds(j, 1), :] = (freqs[j] * sample) % nfft
+        return carry
+
+    lax.fori_loop(0, nf, phase_row, 0)
+    angle_val = 2.0 * math.pi / nfft * phase[...].astype(F32)
+    window = 0.5 - 0.5 * jnp.cos(2.0 * math.pi / nfft * sample.astype(F32))
+    norm_scale = 2.0 / math.sqrt(nfft)
+    table[:nf, :] = (window * jnp.cos(angle_val) * norm_scale).astype(BF16)
+    table[nf:, :] = (-window * jnp.sin(angle_val) * norm_scale).astype(BF16)
 
 
 def round_up(value, step):
@@ -46,8 +52,8 @@
     return lane % nf == row
 
 
-def exchange_kernel(dims, x_ref, starts_ref, table_ref, spec_ref, cross_ref,
-                    arrived, w_ref, spec, gram, rows_a, rows_b, slots_ta, slots_ga,
+def exchange_kernel(dims, x_ref, starts_hbm, freqs_hbm, spec_ref, cross_ref,
+                    starts_ref, freqs_ref, small_sem, phase, table_ref, arrived, w_ref, spec, gram, rows_a, rows_b, slots_ta, slots_ga,
                     send_sem, recv_sem, own_sem, out_sem, sa_sem, ra_sem, sb_sem, rb_sem):
     n, nz, nb, nf, pts, chunks = dims
     me = lax.axis_index("ta")
@@ -92,6 +98,14 @@
             piece(k, o).start()
         own(k).start()
 
+    fetch_starts = pltpu.make_async_copy(starts_hbm, starts_ref, small_sem.at[0])
+    fetch_freqs = pltpu.make_async_copy(freqs_hbm, freqs_ref, small_sem.at[1])
+    fetch_starts.start()
+    fetch_freqs.start()
+    fetch_starts.wait()
+    fetch_freqs.wait()
+    build_table(phase, freqs_ref, table_ref)
+
     total_times = n * times
     lag = (lax.broadcasted_iota(jnp.int32, (NFFT, total_times), 1)
            - lax.broadcasted_iota(jnp.int32, (NFFT, total_times), 0))
@@ -175,7 +189,7 @@
         stage_b(o).wait_send()
 
 
-def power_kernel(dims, scale, cross_ref, spec_ref, spec_out, power_out, high, low):
+def power_kernel(dims, scale, cross_ref, spec_ref, spec_out, power_out, mix):
     nb, nf = dims
     rows = nb * 2 * nf
     lanes = cross_ref.shape[1]
@@ -189,15 +203,12 @@
         for b in range(nb):
             for c, source in enumerate((cross, turned)):
                 m = jnp.where(keep, jnp.broadcast_to(source[b:b + 1, :], (nf, lanes)), 0.0)[:, :rows]
-                hi = m.astype(BF16)
                 r0 = (2 * b + c) * nf
-                high[r0:r0 + nf, :] = hi
-                low[r0:r0 + nf, :] = (m - hi.astype(F32)).astype(BF16)
+                mix[r0:r0 + nf, :] = m.astype(BF16)
 
     s = spec_ref[...]
     spec_out[...] = s
-    power_out[...] = (jnp.dot(high[...], s, preferred_element_type=F32)
-                      + jnp.dot(low[...], s, preferred_element_type=F32))
+    power_out[...] = jnp.dot(mix[...], s, preferred_element_type=F32)
 
 
 def shards(snapshots, block_starts, kept_freqs):
@@ -213,18 +224,21 @@
     width = pts // 4
     chunks = [(c0, width) for c0 in range(0, pts, width)]
     nk = len(chunks)
-    table = kernel_table(kept_freqs, jnp.arange(NFFT, dtype=jnp.int32)).astype(BF16)
-    x = snapshots.reshape(times, snapshots.shape[2])
+    operands = [pltpu.with_memory_space_constraint(a, pltpu.HBM) for a in (
+        snapshots.reshape(times, snapshots.shape[2]), block_starts, kept_freqs)]
     dma = pltpu.SemaphoreType.DMA
     spectra, cross = pl.pallas_call(
         functools.partial(exchange_kernel, (n, nz, nb, nf, pts, chunks)),
         out_shape=(jax.ShapeDtypeStruct((rows, pts), BF16),
                    jax.ShapeDtypeStruct((8, lanes), F32)),
-        in_specs=[pl.BlockSpec(memory_space=pltpu.HBM),
-                  pl.BlockSpec(memory_space=pltpu.SMEM),
-                  pl.BlockSpec(memory_space=pltpu.VMEM)],
+        in_specs=[pl.BlockSpec(memory_space=pl.ANY)] * 3,
         out_specs=(pl.BlockSpec(memory_space=pl.ANY), pl.BlockSpec(memory_space=pltpu.VMEM)),
         scratch_shapes=[
+            pltpu.SMEM((nb,), jnp.int32),
+            pltpu.SMEM((nf,), jnp.int32),
+            dma((2,)),
+            pltpu.VMEM((nf, NFFT), jnp.int32),
+            pltpu.VMEM((2 * nf, NFFT), BF16),
             pltpu.VMEM((n * times, pts), BF16),
             pltpu.VMEM((rows, n * times), BF16),
             pltpu.VMEM((rows, pts), BF16),
@@ -239,7 +253,7 @@
         compiler_params=pltpu.CompilerParams(
             collective_id=0, has_side_effects=True, vmem_limit_bytes=40 * 1024 * 1024),
         name="exchange",
-    )(x, block_starts, table)
+    )(*operands)
 
     tile = pts // 4
     spectra, power = pl.pallas_call(
@@ -251,7 +265,7 @@
                   pl.BlockSpec((rows, tile), lambda i: (0, i))],
         out_specs=(pl.BlockSpec((rows, tile), lambda i: (0, i)),
                    pl.BlockSpec((rows, tile), lambda i: (0, i))),
-        scratch_shapes=[pltpu.VMEM((rows, rows), BF16), pltpu.VMEM((rows, rows), BF16)],
+        scratch_shapes=[pltpu.VMEM((rows, rows), BF16)],
         compiler_params=pltpu.CompilerParams(vmem_limit_bytes=32 * 1024 * 1024),
         name="power",
     )(cross, spectra)

time: 70.5 us -> 65.7 us (0.932)
  local copies, waits for them, and re-layouts: 2.84 us -> 0 us
  Pallas kernels: 65.9 us -> 64.9 us
  other arithmetic: 0.93 us -> 0 us
    unnamed x4 -> x0, local copies, waits for them, and re-layouts: 2.84 us -> none
    another operation x1 -> x0, other arithmetic: 0.87 us -> none
    pallas_call x1, Pallas kernels: 4.1 us -> 3.34 us  [shards(): pl.pallas_call(functools.partial(power_kernel, (nb, nf), 1.0 / float(nb *...]
where the time goes in v2:
time: 65.7 us; the launch traced here: 65.5 us
  Pallas kernels  64.9 us (99%)
    pallas_call x1, Pallas kernels, shards(): pl.pallas_call(functools.partial(exchange_kernel, (n, nz, nb, nf, pts, ch...  61.5 us
    pallas_call x1, Pallas kernels, shards(): pl.pallas_call(functools.partial(power_kernel, (nb, nf), 1.0 / float(nb *...  3.34 us

profile of v2, /device:TPU:0, one launch (start us, length us, event | category | flops | bytes accessed | tf_op | source)
XLA Modules:
  0.0 65.5 jit_solution(17738797505505534171)
XLA Ops:
  0.6 61.5 %exchange.1 = (bf16[448,2048]{1,0:T(8,128)(2,1)S(1)}, f32[8,512]{1,0:T(8,128)S(1)}) custom-call(bf16[128,16384]{1,0:T(8,128)(2,1)} %bitcast.3, s32[7]{0:T(128)} %starts_hbm.1, s32[32]{0:T(128)} %freqs_hbm.1), custom_call_target="tpu_custom_call" | custom-call | tf_op jit(solution)/shard_map/exchange/pallas_call | solution.py:230
  62.2 3.3 %power.1 = (bf16[448,2048]{1,0:T(8,128)(2,1)}, f32[448,2048]{1,0:T(8,128)}) custom-call(f32[8,512]{1,0:T(8,128)S(1)} %get-tuple-element.6.cross_ref, bf16[448,2048]{1,0:T(8,128)(2,1)S(1)} %get-tuple-element.7.spec_ref), custom_call_target="tpu_custom_call" | custom-call | tf_op jit(solution)/shard_map/power/pallas_call | solution.py:259

commit v3 on v2

--- a/solution.py
+++ b/solution.py
@@ -52,9 +52,126 @@
     return lane % nf == row
 
 
+def direct_plan(n, pts, chunks, x_ref, arrived, send_sem, recv_sem):
+    me = lax.axis_index("ta")
+    mz = lax.axis_index("ga")
+    times = x_ref.shape[0]
+    every = [(k, o) for k in range(len(chunks)) for o in range(1, n)]
+
+    def piece(k, o):
+        c0, cw = chunks[k]
+        peer = lax.rem(me + o, n)
+        return pltpu.make_async_remote_copy(
+            src_ref=x_ref.at[:, pl.ds(pl.multiple_of(peer * pts + c0, 128), cw)],
+            dst_ref=arrived.at[pl.ds(pl.multiple_of(me * times, times), times), pl.ds(c0, cw)],
+            send_sem=send_sem.at[k, o],
+            recv_sem=recv_sem.at[k, o],
+            device_id=(peer, mz),
+            device_id_type=MESH,
+        )
+
+    def begin():
+        for k, o in every:
+            piece(k, o).start()
+
+    def follow():
+        pass
+
+    def receive(k):
+        for o in range(1, n):
+            piece(k, o).wait_recv()
+
+    def finish():
+        for k, o in every:
+            piece(k, o).wait_send()
+
+    return begin, follow, receive, finish
+
+
+def square_plan(pts, chunks, x_ref, arrived, relay, send_sem, recv_sem):
+    me = lax.axis_index("ta")
+    mz = lax.axis_index("ga")
+    times = x_ref.shape[0]
+    core, x, y = me % 2, (me // 2) % 2, me // 4
+    count = range(len(chunks))
+
+    def index(yy, xx, cc):
+        return (yy * 2 + xx) * 2 + cc
+
+    def copy(k, src, dst, slot_out, slot_in, device):
+        return pltpu.make_async_remote_copy(
+            src_ref=src, dst_ref=dst, send_sem=send_sem.at[k, slot_out], recv_sem=recv_sem.at[k, slot_in],
+            device_id=(device, mz), device_id_type=MESH)
+
+    def columns(k, owner):
+        c0, cw = chunks[k]
+        return x_ref.at[:, pl.ds(pl.multiple_of(owner * pts + c0, 128), cw)]
+
+    def place(k, source):
+        c0, cw = chunks[k]
+        return arrived.at[pl.ds(pl.multiple_of(source * times, times), times), pl.ds(c0, cw)]
+
+    def to_relay(k, c):
+        c0, cw = chunks[k]
+        return copy(k, columns(k, index(1 - y, 1 - x, c)), relay.at[c, :, pl.ds(c0, cw)],
+                    c, c, index(y, 1 - x, core))
+
+    def along_x(k, c):
+        peer = index(y, 1 - x, c)
+        return copy(k, columns(k, peer), place(k, me), 2 + c, 2 + core, peer)
+
+    def along_y(k, c):
+        peer = index(1 - y, x, c)
+        return copy(k, columns(k, peer), place(k, me), 4 + c, 4 + core, peer)
+
+    def onward(k, c):
+        c0, cw = chunks[k]
+        return copy(k, relay.at[c, :, pl.ds(c0, cw)], place(k, index(y, 1 - x, core)),
+                    7 + c, 7 + core, index(1 - y, x, c))
+
+    def across(k):
+        peer = index(y, x, 1 - core)
+        return copy(k, columns(k, peer), place(k, me), 6, 6, peer)
+
+    def arrival(k, slot):
+        return copy(k, place(k, me), place(k, me), slot, slot, me)
+
+    def begin():
+        for k in count:
+            for c in range(2):
+                to_relay(k, c).start()
+                along_y(k, c).start()
+        for k in count:
+            across(k).start()
+
+    def follow():
+        for k in count:
+            for c in range(2):
+                to_relay(k, c).wait_recv()
+                onward(k, c).start()
+            for c in range(2):
+                along_x(k, c).start()
+
+    def receive(k):
+        across(k).wait_recv()
+        for slot in (2, 3, 4, 5, 7, 8):
+            arrival(k, slot).wait_recv()
+
+    def finish():
+        for k in count:
+            for c in range(2):
+                to_relay(k, c).wait_send()
+                along_x(k, c).wait_send()
+                along_y(k, c).wait_send()
+                onward(k, c).wait_send()
+            across(k).wait_send()
+
+    return begin, follow, receive, finish
+
+
 def exchange_kernel(dims, x_ref, starts_hbm, freqs_hbm, spec_ref, cross_ref,
                     starts_ref, freqs_ref, small_sem, phase, table_ref, arrived, w_ref, spec, gram, rows_a, rows_b, slots_ta, slots_ga,
-                    send_sem, recv_sem, own_sem, out_sem, sa_sem, ra_sem, sb_sem, rb_sem):
+                    send_sem, recv_sem, own_sem, out_sem, sa_sem, ra_sem, sb_sem, rb_sem, relay=None):
     n, nz, nb, nf, pts, chunks = dims
     me = lax.axis_index("ta")
     mz = lax.axis_index("ga")
@@ -69,19 +186,11 @@
         pl.semaphore_signal(barrier, inc=1, device_id=(me, lax.rem(mz + o, nz)), device_id_type=MESH)
     pl.semaphore_wait(barrier, n - 1 + nz - 1)
 
-    def piece(k, o):
-        c0, cw = chunks[k]
-        peer = lax.rem(me + o, n)
-        src_col = pl.multiple_of(peer * pts + c0, 128)
-        dst_row = pl.multiple_of(me * times, times)
-        return pltpu.make_async_remote_copy(
-            src_ref=x_ref.at[:, pl.ds(src_col, cw)],
-            dst_ref=arrived.at[pl.ds(dst_row, times), pl.ds(c0, cw)],
-            send_sem=send_sem.at[k, o],
-            recv_sem=recv_sem.at[k, o],
-            device_id=(peer, mz),
-            device_id_type=MESH,
-        )
+    if relay is None:
+        plan = direct_plan(n, pts, chunks, x_ref, arrived, send_sem, recv_sem)
+    else:
+        plan = square_plan(pts, chunks, x_ref, arrived, relay, send_sem, recv_sem)
+    begin, follow, receive, finish = plan
 
     def own(k):
         c0, cw = chunks[k]
@@ -93,9 +202,8 @@
             own_sem.at[k],
         )
 
+    begin()
     for k in range(len(chunks)):
-        for o in order:
-            piece(k, o).start()
         own(k).start()
 
     fetch_starts = pltpu.make_async_copy(starts_hbm, starts_ref, small_sem.at[0])
@@ -121,6 +229,8 @@
     rows_a[...] = jnp.zeros_like(rows_a)
     rows_b[...] = jnp.zeros_like(rows_b)
 
+    follow()
+
     def out_copy(k):
         c0, cw = chunks[k]
         return pltpu.make_async_copy(
@@ -128,8 +238,7 @@
 
     for k, (c0, cw) in enumerate(chunks):
         own(k).wait()
-        for o in order:
-            piece(k, o).wait_recv()
+        receive(k)
         s = jnp.dot(w_ref[...], arrived[:, c0:c0 + cw], preferred_element_type=F32).astype(BF16)
         spec[:, c0:c0 + cw] = s
         out_copy(k).start()
@@ -181,8 +290,7 @@
 
     for k in range(len(chunks)):
         out_copy(k).wait()
-        for o in order:
-            piece(k, o).wait_send()
+    finish()
     for o in order:
         stage_a(o).wait_send()
     for o in range(1, nz):
@@ -221,8 +329,9 @@
     rows = nb * 2 * nf
     lanes = round_up(rows, 128)
     assert nb <= 8
-    width = pts // 4
-    chunks = [(c0, width) for c0 in range(0, pts, width)]
+    square = n == 8
+    width = pts // 8
+    chunks = [(0, 2 * width), (2 * width, 2 * width), (4 * width, 2 * width), (6 * width, width), (7 * width, width)]
     nk = len(chunks)
     operands = [pltpu.with_memory_space_constraint(a, pltpu.HBM) for a in (
         snapshots.reshape(times, snapshots.shape[2]), block_starts, kept_freqs)]
@@ -247,9 +356,9 @@
             pltpu.VMEM((8, lanes), F32),
             pltpu.VMEM((n, 8, lanes), F32),
             pltpu.VMEM((nz, 8, lanes), F32),
-            dma((nk, n)), dma((nk, n)), dma((nk,)), dma((nk,)),
+            dma((nk, max(n, 9))), dma((nk, max(n, 9))), dma((nk,)), dma((nk,)),
             dma((n,)), dma((n,)), dma((nz,)), dma((nz,)),
-        ],
+        ] + ([pltpu.VMEM((2, times, pts), BF16)] if square else []),
         compiler_params=pltpu.CompilerParams(
             collective_id=0, has_side_effects=True, vmem_limit_bytes=40 * 1024 * 1024),
         name="exchange",

time: 65.7 us -> 65.8 us (level)
  no operation moved by 1% of the time
where the time goes in v3:
time: 65.8 us; the launch traced here: 65.6 us
  Pallas kernels  65 us (99%)
    pallas_call x1, Pallas kernels, shards(): pl.pallas_call(functools.partial(exchange_kernel, (n, nz, nb, nf, pts, ch...  61.7 us
    pallas_call x1, Pallas kernels, shards(): pl.pallas_call(functools.partial(power_kernel, (nb, nf), 1.0 / float(nb *...  3.33 us

profile of v3, /device:TPU:0, one launch (start us, length us, event | category | flops | bytes accessed | tf_op | source)
XLA Modules:
  0.0 65.6 jit_solution(12743596408777385168)
XLA Ops:
  0.6 61.7 %exchange.1 = (bf16[448,2048]{1,0:T(8,128)(2,1)S(1)}, f32[8,512]{1,0:T(8,128)S(1)}) custom-call(bf16[128,16384]{1,0:T(8,128)(2,1)} %bitcast.3, s32[7]{0:T(128)} %starts_hbm.1, s32[32]{0:T(128)} %freqs_hbm.1), custom_call_target="tpu_custom_call" | custom-call | tf_op jit(solution)/shard_map/exchange/pallas_call | solution.py:339
  62.3 3.3 %power.1 = (bf16[448,2048]{1,0:T(8,128)(2,1)}, f32[448,2048]{1,0:T(8,128)}) custom-call(f32[8,512]{1,0:T(8,128)S(1)} %get-tuple-element.6.cross_ref, bf16[448,2048]{1,0:T(8,128)(2,1)S(1)} %get-tuple-element.7.spec_ref), custom_call_target="tpu_custom_call" | custom-call | tf_op jit(solution)/shard_map/power/pallas_call | solution.py:368

commit v4 on v3

--- a/solution.py
+++ b/solution.py
@@ -9,6 +9,7 @@
 from jax.sharding import PartitionSpec as P
 
 NFFT = 256
+POWER_TILES = 2
 MESH = pl.DeviceIdType.MESH
 F32 = jnp.float32
 BF16 = jnp.bfloat16
@@ -255,7 +256,7 @@
     swapped = swap_halves(rows_b[...], nf)
     local = rows_a[...] + jnp.where(half_mask(nf, lanes), swapped, -swapped)
 
-    slots_ta[me] = local
+    slots_ta[me] = local.astype(BF16)
 
     def stage_a(o):
         peer = lax.rem(me + o, n)
@@ -275,17 +276,17 @@
         stage_a(o).start()
     for o in order:
         stage_a(o).wait_recv()
-    plane = slots_ta[0]
+    plane = slots_ta[0].astype(F32)
     for i in range(1, n):
-        plane = plane + slots_ta[i]
-    slots_ga[mz] = plane
+        plane = plane + slots_ta[i].astype(F32)
+    slots_ga[mz] = plane.astype(BF16)
     for o in range(1, nz):
         stage_b(o).start()
     for o in range(1, nz):
         stage_b(o).wait_recv()
-    whole = slots_ga[0]
+    whole = slots_ga[0].astype(F32)
     for i in range(1, nz):
-        whole = whole + slots_ga[i]
+        whole = whole + slots_ga[i].astype(F32)
     cross_ref[...] = whole
 
     for k in range(len(chunks)):
@@ -297,26 +298,33 @@
         stage_b(o).wait_send()
 
 
-def power_kernel(dims, scale, cross_ref, spec_ref, spec_out, power_out, mix):
-    nb, nf = dims
-    rows = nb * 2 * nf
+def power_kernel(dims, scale, cross_ref, spec_ref, spec_out, power_out, mix, result, spec_sem, tile_sem):
+    nb, nf, tile = dims
+    rows, pts = spec_ref.shape
     lanes = cross_ref.shape[1]
-
-    @pl.when(pl.program_id(0) == 0)
-    def _():
-        cross = cross_ref[...] * scale
-        swapped = swap_halves(cross, nf)
-        turned = jnp.where(half_mask(nf, lanes), -swapped, swapped)
-        keep = diagonal(nf, lanes)
-        for b in range(nb):
-            for c, source in enumerate((cross, turned)):
-                m = jnp.where(keep, jnp.broadcast_to(source[b:b + 1, :], (nf, lanes)), 0.0)[:, :rows]
-                r0 = (2 * b + c) * nf
-                mix[r0:r0 + nf, :] = m.astype(BF16)
-
-    s = spec_ref[...]
-    spec_out[...] = s
-    power_out[...] = jnp.dot(mix[...], s, preferred_element_type=F32)
+    spectra_copy = pltpu.make_async_copy(spec_ref, spec_out, spec_sem)
+    spectra_copy.start()
+    cross = cross_ref[...] * scale
+    swapped = swap_halves(cross, nf)
+    turned = jnp.where(half_mask(nf, lanes), -swapped, swapped)
+    keep = diagonal(nf, lanes)
+    for b in range(nb):
+        for c, source in enumerate((cross, turned)):
+            m = jnp.where(keep, jnp.broadcast_to(source[b:b + 1, :], (nf, lanes)), 0.0)[:, :rows]
+            r0 = (2 * b + c) * nf
+            mix[r0:r0 + nf, :] = m.astype(BF16)
+
+    def tile_copy(i):
+        part = pl.ds(i * tile, tile)
+        return pltpu.make_async_copy(result.at[:, part], power_out.at[:, part], tile_sem.at[i])
+
+    for i in range(pts // tile):
+        result[:, i * tile:(i + 1) * tile] = jnp.dot(
+            mix[...], spec_ref[:, i * tile:(i + 1) * tile], preferred_element_type=F32)
+        tile_copy(i).start()
+    for i in range(pts // tile):
+        tile_copy(i).wait()
+    spectra_copy.wait()
 
 
 def shards(snapshots, block_starts, kept_freqs):
@@ -354,8 +362,8 @@
             pltpu.VMEM((rows, lanes), F32),
             pltpu.VMEM((8, lanes), F32),
             pltpu.VMEM((8, lanes), F32),
-            pltpu.VMEM((n, 8, lanes), F32),
-            pltpu.VMEM((nz, 8, lanes), F32),
+            pltpu.VMEM((n, 8, lanes), BF16),
+            pltpu.VMEM((nz, 8, lanes), BF16),
             dma((nk, max(n, 9))), dma((nk, max(n, 9))), dma((nk,)), dma((nk,)),
             dma((n,)), dma((n,)), dma((nz,)), dma((nz,)),
         ] + ([pltpu.VMEM((2, times, pts), BF16)] if square else []),
@@ -364,17 +372,15 @@
         name="exchange",
     )(*operands)
 
-    tile = pts // 4
+    tile = pts // POWER_TILES
     spectra, power = pl.pallas_call(
-        functools.partial(power_kernel, (nb, nf), 1.0 / float(nb * pts * n * nz)),
-        grid=(pts // tile,),
+        functools.partial(power_kernel, (nb, nf, tile), 1.0 / float(nb * pts * n * nz)),
         out_shape=(jax.ShapeDtypeStruct((rows, pts), BF16),
                    jax.ShapeDtypeStruct((rows, pts), F32)),
-        in_specs=[pl.BlockSpec((8, lanes), lambda i: (0, 0)),
-                  pl.BlockSpec((rows, tile), lambda i: (0, i))],
-        out_specs=(pl.BlockSpec((rows, tile), lambda i: (0, i)),
-                   pl.BlockSpec((rows, tile), lambda i: (0, i))),
-        scratch_shapes=[pltpu.VMEM((rows, rows), BF16)],
+        in_specs=[pl.BlockSpec(memory_space=pltpu.VMEM)] * 2,
+        out_specs=(pl.BlockSpec(memory_space=pltpu.HBM), pl.BlockSpec(memory_space=pltpu.HBM)),
+        scratch_shapes=[pltpu.VMEM((rows, rows), BF16), pltpu.VMEM((rows, pts), F32),
+                        dma(()), dma((pts // tile,))],
         compiler_params=pltpu.CompilerParams(vmem_limit_bytes=32 * 1024 * 1024),
         name="power",
     )(cross, spectra)

time: 65.8 us -> 64.4 us (0.979)
  Pallas kernels: 65 us -> 63.6 us
    pallas_call x1, Pallas kernels: 3.33 us -> 2.55 us  [shards(): pl.pallas_call(functools.partial(power_kernel, (nb, nf, tile), 1.0 / floa...]
where the time goes in v4:
time: 64.4 us; the launch traced here: 64.3 us
  Pallas kernels  63.6 us (99%)
    pallas_call x1, Pallas kernels, shards(): pl.pallas_call(functools.partial(exchange_kernel, (n, nz, nb, nf, pts, ch...  61.1 us
    pallas_call x1, Pallas kernels, shards(): pl.pallas_call(functools.partial(power_kernel, (nb, nf, tile), 1.0 / floa...  2.55 us

profile of v4, /device:TPU:0, one launch (start us, length us, event | category | flops | bytes accessed | tf_op | source)
XLA Modules:
  0.0 64.3 jit_solution(14981784995152586723)
XLA Ops:
  0.6 61.1 %exchange.1 = (bf16[448,2048]{1,0:T(8,128)(2,1)S(1)}, f32[8,512]{1,0:T(8,128)S(1)}) custom-call(bf16[128,16384]{1,0:T(8,128)(2,1)} %bitcast.3, s32[7]{0:T(128)} %starts_hbm.1, s32[32]{0:T(128)} %freqs_hbm.1), custom_call_target="tpu_custom_call" | custom-call | tf_op jit(solution)/shard_map/exchange/pallas_call | solution.py:347
  61.7 2.6 %power.1 = (bf16[448,2048]{1,0:T(8,128)(2,1)}, f32[448,2048]{1,0:T(8,128)}) custom-call(f32[8,512]{1,0:T(8,128)S(1)} %get-tuple-element.6.cross_ref, bf16[448,2048]{1,0:T(8,128)(2,1)S(1)} %get-tuple-element.7.spec_ref), custom_call_target="tpu_custom_call" | custom-call | tf_op jit(solution)/shard_map/power/pallas_call | solution.py:376

commit v5 on v4

--- a/solution.py
+++ b/solution.py
@@ -339,7 +339,7 @@
     assert nb <= 8
     square = n == 8
     width = pts // 8
-    chunks = [(0, 2 * width), (2 * width, 2 * width), (4 * width, 2 * width), (6 * width, width), (7 * width, width)]
+    chunks = [(0, 2 * width), (2 * width, 2 * width), (4 * width, 2 * width), (6 * width, 2 * width)]
     nk = len(chunks)
     operands = [pltpu.with_memory_space_constraint(a, pltpu.HBM) for a in (
         snapshots.reshape(times, snapshots.shape[2]), block_starts, kept_freqs)]

time: 64.4 us -> 63.9 us (level)
  no operation moved by 1% of the time
where the time goes in v5:
time: 63.9 us; the launch traced here: 63.8 us
  Pallas kernels  63.1 us (99%)
  between operations  0.64 us (1%)
    pallas_call x1, Pallas kernels, shards(): pl.pallas_call(functools.partial(exchange_kernel, (n, nz, nb, nf, pts, ch...  60.6 us
    pallas_call x1, Pallas kernels, shards(): pl.pallas_call(functools.partial(power_kernel, (nb, nf, tile), 1.0 / floa...  2.55 us

profile of v5, /device:TPU:0, one launch (start us, length us, event | category | flops | bytes accessed | tf_op | source)
XLA Modules:
  0.0 63.8 jit_solution(8987094970299303930)
XLA Ops:
  0.6 60.6 %exchange.1 = (bf16[448,2048]{1,0:T(8,128)(2,1)S(1)}, f32[8,512]{1,0:T(8,128)S(1)}) custom-call(bf16[128,16384]{1,0:T(8,128)(2,1)} %bitcast.3, s32[7]{0:T(128)} %starts_hbm.1, s32[32]{0:T(128)} %freqs_hbm.1), custom_call_target="tpu_custom_call" | custom-call | tf_op jit(solution)/shard_map/exchange/pallas_call | solution.py:347
  61.2 2.6 %power.1 = (bf16[448,2048]{1,0:T(8,128)(2,1)}, f32[448,2048]{1,0:T(8,128)}) custom-call(f32[8,512]{1,0:T(8,128)S(1)} %get-tuple-element.6.cross_ref, bf16[448,2048]{1,0:T(8,128)(2,1)S(1)} %get-tuple-element.7.spec_ref), custom_call_target="tpu_custom_call" | custom-call | tf_op jit(solution)/shard_map/power/pallas_call | solution.py:376
